TPU v7x, 32 devices: a whole 2x2x4 slice. The times are simulated.
32 devices in a mesh: actor: 8 (over z, x), mp: 4 (over y, core).
Axes of the slice: x: 2, y: 2, z: 4, core: 2. Of those that a mesh axis runs over, the one named last changes fastest.
Arguments:
- resid: bfloat16 [8192, 4096], P('actor')
- norm_gain: bfloat16 [4096], replicated, may hold values from 0.25 to 1.75
- query_weight: bfloat16 [4096, 4096], P(None, 'mp'), may hold values from -0.09375 to 0.09375
- cotangent: bfloat16 [8192, 4096], P('actor', 'mp'), may hold values from -0.875 to 0.875
- lengths: int32 [32], P('actor'), may hold values from 1 to 256
- owner: int32 [8], replicated, may hold values from 0 to 7, each once
- adapter_table: float32 [4, 8, 128, 128], P('mp', 'actor')
- moment_one: float32 [4, 8, 128, 128], P('mp', 'actor'), may hold values from -3 to 3
- moment_two: float32 [4, 8, 128, 128], P('mp', 'actor'), may hold values from 0.003 to 0.1
Outputs:
- query: bfloat16 [8192, 4096], P('actor', 'mp')
- adapter_new: float32 [4, 8, 128, 128], P('mp', 'actor')
- moment_one_new: float32 [4, 8, 128, 128], P('mp', 'actor')
- moment_two_new: float32 [4, 8, 128, 128], P('mp', 'actor')
- merged: bfloat16 [4096, 4096], P('actor', 'mp')
Inputs may be any that keep to these rules, and one draw needn't show every extreme that they name: owner is a permutation: every actor keeps exactly one block of each feature slice.
All inputs are finite; a program needn't handle non-finite values.
Results may differ from a plain program's by a relative error of at most 0.0064.
Values may be sent and summed in bfloat16 or wider, within the bound.
A program may use at most 128 MiB of HBM per device.

v0:
```python
import jax
import jax.numpy as jnp
from jax import lax
from jax.sharding import PartitionSpec as P

LEN = 256


adapter_scale = 0.5
learn_rate = 0.003
beta_one = 0.9
beta_two = 0.999
fix_one = 1.0 - 0.9**10
fix_two = 1.0 - 0.999**10


def contracted_rows(left, right):
    return lax.dot_general(
        left, right, (((0,), (0,)), ((), ())), preferred_element_type=jnp.float32
    )


def contracted_columns(left, right):
    return lax.dot_general(
        left, right, (((1,), (1,)), ((), ())), preferred_element_type=jnp.float32
    )


def rebuild(gathered, owner, n_actor, n_mp):
    blocks = gathered.reshape(
        n_actor, n_mp, gathered.shape[0] // (n_actor * n_mp), gathered.shape[1]
    )
    ordered = jnp.take(blocks, owner, axis=0)
    return jnp.transpose(ordered, (1, 0, 2, 3)).reshape(-1, gathered.shape[1])


def slice_rows(gathered, owner, n_actor):
    block = gathered.shape[0] // n_actor
    ordered = jnp.take(gathered.reshape(n_actor, block, gathered.shape[1]), owner, axis=0)
    return ordered.reshape(n_actor * block, gathered.shape[1])


def body(
    resid, norm_gain, query_weight, cotangent, lengths, owner, adapter_table, moment_one, moment_two
):
    n_actor = lax.axis_size("actor")
    n_mp = lax.axis_size("mp")
    mp_index = lax.axis_index("mp")
    actor_index = lax.axis_index("actor")
    tokens = resid.shape[0]
    width = resid.shape[1]
    cols = query_weight.shape[1]
    block = adapter_table.shape[2]
    rank = adapter_table.shape[3] // 2
    stream = resid.astype(jnp.float32)
    meansq = jnp.mean(stream * stream, axis=1, keepdims=True)
    normalized_input = (
        stream * lax.rsqrt(meansq + 1e-05) * norm_gain.astype(jnp.float32)[None, :]
    ).astype(jnp.bfloat16)
    index = jnp.arange(tokens, dtype=jnp.int32)
    position = index % LEN
    sequence = index // LEN
    seq_ids = jnp.arange(lengths.shape[0], dtype=jnp.int32)
    active_rows = jnp.any(
        (sequence[:, None] == seq_ids[None, :]) & (position[:, None] < lengths[None, :]), axis=1
    )
    masked_rows = jnp.where(active_rows[:, None], cotangent, jnp.zeros_like(cotangent))
    normalized_local = lax.dynamic_slice_in_dim(normalized_input, mp_index * cols, cols, 1)
    now_shard = adapter_table.reshape(block, 2 * rank).astype(jnp.bfloat16)
    part = lax.all_gather(now_shard, "actor", axis=0, tiled=True)
    mine = slice_rows(part, owner, n_actor)
    bt_mine = mine[:, rank:]
    low_part = jnp.dot(normalized_local, mine[:, :rank], preferred_element_type=jnp.float32)
    back_part = jnp.dot(masked_rows, bt_mine, preferred_element_type=jnp.float32)
    low_sum, back_sum = lax.psum((low_part.reshape(-1, 128), back_part.reshape(-1, 128)), "mp")
    low_full = low_sum.reshape(tokens, rank)
    back_full = back_sum.reshape(tokens, rank)
    lowrank_output = low_full.astype(jnp.bfloat16)
    backward_rows = back_full.astype(jnp.bfloat16)
    base_output = jnp.dot(normalized_input, query_weight, preferred_element_type=jnp.float32)
    extra_term = contracted_columns(lowrank_output, bt_mine)
    query = jnp.where(active_rows[:, None], base_output + adapter_scale * extra_term, 0.0).astype(
        jnp.bfloat16
    )
    down_gradient = adapter_scale * contracted_rows(normalized_local, backward_rows)
    up_transposed_gradient = adapter_scale * contracted_rows(masked_rows, lowrank_output)
    grad = jnp.concatenate([down_gradient, up_transposed_gradient], axis=1)
    actors = jnp.arange(n_actor, dtype=jnp.int32)
    inverse = jnp.sum(jnp.where(owner[None, :] == actors[:, None], actors[None, :], 0), axis=1)
    reordered = jnp.take(grad.reshape(n_actor, block, 2 * rank), inverse, axis=0).reshape(
        cols, 2 * rank
    )
    summed = lax.psum_scatter(reordered, "actor", scatter_dimension=0, tiled=True)
    first = beta_one * moment_one.reshape(block, 2 * rank) + (1.0 - beta_one) * summed
    second = beta_two * moment_two.reshape(block, 2 * rank) + (1.0 - beta_two) * summed * summed
    updated = adapter_table.reshape(block, 2 * rank) - learn_rate * (first / fix_one) / (
        jnp.sqrt(second / fix_two) + 1e-08
    )
    updated_low = updated.astype(jnp.bfloat16)
    row_count = width // n_actor
    fresh_all = lax.all_gather(updated_low, ("actor", "mp"), axis=0, tiled=True)
    fresh = rebuild(fresh_all, owner, n_actor, n_mp)
    down_matrix_rows = lax.dynamic_slice_in_dim(fresh, actor_index * row_count, row_count, 0)[
        :, :rank
    ]
    up_transposed_columns = lax.dynamic_slice_in_dim(fresh, mp_index * cols, cols, 0)[:, rank:]
    weight_rows = lax.dynamic_slice_in_dim(query_weight, actor_index * row_count, row_count, 0)
    merged = (
        weight_rows.astype(jnp.float32)
        + adapter_scale * contracted_columns(down_matrix_rows, up_transposed_columns)
    ).astype(jnp.bfloat16)
    shape = adapter_table.shape
    return (query, updated.reshape(shape), first.reshape(shape), second.reshape(shape), merged)


def solution(mesh):
    return jax.shard_map(
        body,
        mesh=mesh,
        in_specs=(
            P("actor", None),
            P(),
            P(None, "mp"),
            P("actor", "mp"),
            P("actor"),
            P(),
            P("mp", "actor", None, None),
            P("mp", "actor", None, None),
            P("mp", "actor", None, None),
        ),
        out_specs=(
            P("actor", "mp"),
            P("mp", "actor", None, None),
            P("mp", "actor", None, None),
            P("mp", "actor", None, None),
            P("actor", "mp"),
        ),
        check_vma=False,
    )
```

profile of v0, /device:TPU:0, one launch (start us, length us, event | category | flops | bytes accessed | tf_op | source)
XLA Modules:
  0.0 218.0 jit_solution(11755096564712108993)
XLA Ops:
  7.2 0.7 compare_and_fusion.1
  7.9 0.8 select_reduce_fusion
  8.7 0.7 compare_select_fusion.2
  9.5 5.1 %fusion = f32[1024]{0:T(1024)S(1)} fusion(bf16[1024,4096]{1,0:T(8,128)(2,1)} %param.9), kind=kLoop, calls=%fused_computation.5 | loop fusion | flops 12581888 | bytes 8392704 | tf_op jit(solution)/shard_map/reduce_sum | solution.py:56
  14.7 32.6 %all_gather.6 = bf16[1024,128]{1,0:T(8,128)(2,1)S(1)} all-gather(bf16[128,128]{1,0:T(8,128)(2,1)S(1)} %bitcast_convert_fusion), channel_id=1, replica_groups=mesh['actor'=8,'mp'=4] {'actor'}, dimensions={0}, use_global_device_ids=true | all-gather | bytes 294912 | tf_op jit(solution)/shard_map/all_gather | solution.py:70
  47.2 0.6 gather_fusion
  47.8 0.2 bitcast_select_fusion.1
  48.2 2.4 %fusion.10 = f32[1024,64]{1,0:T(8,128)S(1)} fusion(bf16[1024,1024]{1,0:T(8,128)(2,1)} %param.12, pred[1024]{0:T(1024)(128)(4,1)S(1)} %fusion.20, bf16[1024,128]{1,0:T(8,128)(2,1)S(1)} %bitcast_select_fusion.1), kind=kOutput, calls=%fused_computation.18 | convolution fusion | flops 135266304 | bytes 2622464 | tf_op jit(solution)/shard_map/dot_general | solution.py:74
  50.7 10.3 %fusion.2 = bf16[1024,4096]{1,0:T(8,128)(2,1)} fusion(bf16[1024,4096]{1,0:T(8,128)(2,1)} %param.9, f32[4096]{0:T(1024)S(1)} %convert_element_type.37, f32[1024]{0:T(1024)S(1)} %add_rsqrt_fusion), kind=kLoop, calls=%fused_computation.7 | loop fusion | flops 16777216 | bytes 16797696 | tf_op jit(solution)/shard_map/convert_element_type | solution.py:59
  61.0 2.3 %fusion.5 = f32[1024,64]{1,0:T(8,128)S(1)} fusion(bf16[1024,4096]{1,0:T(8,128)(2,1)} %fusion.2, s32[]{:T(128)S(6)} %select_n.82, bf16[1024,128]{1,0:T(8,128)(2,1)S(1)} %bitcast_select_fusion.1), kind=kOutput, calls=%fused_computation.13 | convolution fusion | flops 134217728 | bytes 2621444 | tf_op jit(solution)/shard_map/dot_general | solution.py:73
  63.5 16.4 %all-reduce.2 = (bf16[512,128]{1,0:T(8,128)(2,1)S(1)}, bf16[512,128]{1,0:T(8,128)(2,1)S(1)}) all-reduce(f32[512,128]{1,0:T(8,128)S(1)} %reshape.116, f32[512,128]{1,0:T(8,128)S(1)} %reshape.117), channel_id=1, replica_groups=mesh['actor'=8,'mp'=4] {'mp'}, use_global_device_ids=true, to_apply=%region_2.3 | all-reduce | flops 131072 | bytes 786432 | tf_op jit(solution)/shard_map/psum | solution.py:75
  80.0 2.2 convolution_multiply_fusion
  82.3 2.1 fusion.7
  84.5 0.2 copy.28
  84.7 0.6 gather_fusion.1
  85.3 1.0 bitcast_select_fusion
  86.3 0.2 all-gather.2.cloned.1.call-start
  86.6 63.4 %reduce-scatter.2.cloned.1.call-done = f32[128,128]{1,0:T(8,128)} async-done(((f32[1024,128]{1,0:T(8,128)}), f32[128,128]{1,0:T(8,128)}) %reduce-scatter.2.cloned.1.call-update) | async-done | bytes 65552 | tf_op jit(solution)/shard_map/reduce_scatter | solution.py:93
  150.0 1.6 fusion.34
  151.6 12.6 %fusion.35 = f32[1024,1024]{1,0:T(8,128)S(1)} fusion(bf16[1024,4096]{1,0:T(8,128)(2,1)} %fusion.2, bf16[4096,1024]{1,0:T(8,128)(2,1)} %param.11), kind=kOutput, calls=%fused_computation.67 | convolution fusion | flops 8589934592 | bytes 20971520 | tf_op jit(solution)/shard_map/dot_general | solution.py:80
  164.2 2.1 select_convert_fusion
  166.3 39.8 %all-gather.2.cloned.1.call-done = bf16[4096,128]{1,0:T(8,128)(2,1)} async-done(((bf16[128,128]{1,0:T(8,128)(2,1)}), bf16[4096,128]{1,0:T(8,128)(2,1)}) %all-gather.2.cloned.1.call-update) | async-done | bytes 1048592 | tf_op jit(solution)/shard_map/all_gather | solution.py:101
  206.2 2.0 gather_fusion.2
  208.4 2.7 %add_convert_fusion = bf16[512,1024]{1,0:T(8,128)(2,1)} fusion(bf16[4096,1024]{1,0:T(8,128)(2,1)} %param.11, s32[]{:T(128)S(6)} %select_n.91, bf16[4096,128]{1,0:T(8,128)(2,1)S(1)} %bitcast.47, s32[]{:T(128)S(6)} %select_n.82, s32[]{:T(128)S(6)} %add.93), kind=kOutput, calls=%fused_computation.9 | convolution fusion | flops 69206016 | bytes 2492416 | tf_op jit(solution)/shard_map/dot_general | solution.py:24
  (31 shorter events, 1.2 us)
Async XLA Ops:
  7.2 142.8 %reduce-scatter.2.cloned.1.call-start = ((), (), s32[]{:S(2)}) async-start(), calls=%async_computation.1 | async-start | bytes 589824 | tf_op jit(solution)/shard_map/reduce_scatter | solution.py:93
  9.5 5.2 %copy-start.3 = (bf16[4096]{0:T(1024)(128)(2,1)S(1)}, bf16[4096]{0:T(1024)(128)(2,1)}, u32[]{:S(2)}) copy-start(bf16[4096]{0:T(1024)(128)(2,1)} %param.10) | copy-start | bytes 24580
  9.5 5.2 %copy-start = (f32[1,1,128,128]{3,2,1,0:T(8,128)S(1)}, f32[1,1,128,128]{3,2,1,0:T(8,128)}, u32[]{:S(2)}) copy-start(f32[1,1,128,128]{3,2,1,0:T(8,128)} %param.15) | copy-start | bytes 196612
  9.5 38.5 %copy-start.4 = (s32[4]{0:T(128)S(1)}, s32[4]{0:T(128)}, u32[]{:S(2)}) copy-start(s32[4]{0:T(128)} %param.13) | copy-start | bytes 52
  82.2 67.8 %copy-start.1 = (f32[1,1,128,128]{3,2,1,0:T(8,128)S(1)}, f32[1,1,128,128]{3,2,1,0:T(8,128)}, u32[]{:S(2)}) copy-start(f32[1,1,128,128]{3,2,1,0:T(8,128)} %param.17) | copy-start | bytes 196612
  82.2 67.8 %copy-start.2 = (f32[1,1,128,128]{3,2,1,0:T(8,128)S(1)}, f32[1,1,128,128]{3,2,1,0:T(8,128)}, u32[]{:S(2)}) copy-start(f32[1,1,128,128]{3,2,1,0:T(8,128)} %param.16) | copy-start | bytes 196612
  86.3 119.8 %all-gather.2.cloned.1.call-start = ((), (), s32[]{:S(2)}) async-start(), calls=%async_computation.2 | async-start | bytes 1081344 | tf_op jit(solution)/shard_map/all_gather | solution.py:101
Sparse Core Ops, SparseCore 0:
  86.5 63.4 reduce-scatter.1
  153.4 52.6 all-gather.1
where the time goes:
time: 218 us
  waiting for transfers between devices  103 us (47%)
  blocking collectives  49 us (22%)
  matrix products  26.4 us (12%)
  other arithmetic  20.6 us (9%)
  between operations  14.3 us (7%)
  local copies, waits for them, and re-layouts  4.16 us (2%)
    reduce_scatter x1, waiting for transfers between devices, body(): lax.psum_scatter(reordered, 'actor', scatter_dimension=0, tiled=True)  63.4 us
    all_gather x1, waiting for transfers between devices, body(): fresh_all = lax.all_gather(updated_low, ('actor', 'mp'), axis=0, tiled=True)  39.8 us
    all_gather x1, blocking collectives, body(): part = lax.all_gather(now_shard, 'actor', axis=0, tiled=True)  32.6 us
    psum x1, blocking collectives, body(): lax.psum((low_part.reshape(-1, 128), back_part.reshape(-1, 128)), 'mp')  16.4 us
    dot_general x1, matrix products, body(): jnp.dot(normalized_input, query_weight, preferred_element_type=jnp.float32)  12.6 us
    convert_element_type x1, other arithmetic, body(): normalized_input = (stream * lax.rsqrt(meansq + 1e-05) * norm_gain.astype...  10.3 us
    reduce_sum x1, other arithmetic, body(): meansq = jnp.mean(stream * stream, axis=1, keepdims=True)  5.1 us
    dot_general x2, matrix products, contracted_columns(): lax.dot_general(left, right, (((1,), (1,)), ((), ())), preferred_element_...  4.87 us
  transfers between devices with their start and end apart: 2, of which 2 were waited for; matrix products, arithmetic and copies ran while one was open for 7% of the time, Pallas kernels for 0%

commit v1 on v0

v1 whole, which is shorter than its diff:
```python
import functools

import jax
import jax.numpy as jnp
from jax import lax
from jax.experimental import pallas as pl
from jax.experimental.pallas import tpu as pltpu
from jax.sharding import PartitionSpec as P

MESH = pl.DeviceIdType.MESH
F32 = jnp.float32
BF16 = jnp.bfloat16

adapter_scale = 0.5
learn_rate = 0.003
beta_one = 0.9
beta_two = 0.999
fix_one = 1.0 - 0.9**10
fix_two = 1.0 - 0.999**10

NORM_ROWS = 128
EARLY = 1
MID = 2


def kernel(
    n_actor,
    n_mp,
    lengths,
    owner,
    gain,
    table,
    one,
    two,
    resid,
    weight,
    cotangent,
    query,
    table_new,
    one_new,
    two_new,
    merged,
    x,
    w,
    cot,
    acc,
    qbuf,
    mbuf,
    live,
    gbuf,
    tab,
    pbuf,
    rbuf,
    lb,
    lbr,
    grad,
    sbuf,
    rsbuf,
    nbuf,
    abuf,
    fresh_b,
    fresh_a,
    x_sem,
    w_sem,
    cot_sem,
    q_sem,
    m_sem,
    g_send,
    g_recv,
    p_send,
    p_recv,
    l_send,
    l_recv,
    s_send,
    s_recv,
    n_send,
    n_recv,
    a_send,
    a_recv,
):
    a = lax.axis_index("actor")
    m = lax.axis_index("mp")
    tokens, width = x.shape
    cols = w.shape[1]
    block = table.shape[0]
    lanes = table.shape[1]
    rank = lanes // 2
    nseq = lengths.shape[0]
    seq = tokens // nseq
    part = tokens // n_mp
    share = n_actor // n_mp
    row_count = width // n_actor
    devices = n_actor * n_mp

    norm_steps = tokens // NORM_ROWS

    def x_copy(i):
        rows = pl.ds(pl.multiple_of(i * NORM_ROWS, NORM_ROWS), NORM_ROWS)
        return pltpu.make_async_copy(resid.at[rows], x.at[rows], x_sem.at[i])

    for i in range(norm_steps):
        x_copy(i).start()
    cot_copy = pltpu.make_async_copy(cotangent, cot, cot_sem)
    cot_copy.start()
    w_copy = pltpu.make_async_copy(weight, w, w_sem)
    w_copy.start()

    barrier = pltpu.get_barrier_semaphore()
    me = a * n_mp + m

    @pl.loop(1, devices)
    def _(k):
        other = lax.rem(me + k, devices)
        pl.semaphore_signal(
            barrier, inc=1, device_id=(other // n_mp, lax.rem(other, n_mp)), device_id_type=MESH
        )

    gbuf[0] = table[...].astype(BF16)
    for s in range(nseq):
        live[s * seq : (s + 1) * seq] = jnp.where(
            lax.broadcasted_iota(jnp.int32, (seq, lanes), 0) < lengths[s], 1.0, 0.0
        ).astype(F32)
    pl.semaphore_wait(barrier, devices - 1)

    def to_actor(src, dst, send, recv, k):
        return pltpu.make_async_remote_copy(
            src_ref=src,
            dst_ref=dst,
            send_sem=send.at[k],
            recv_sem=recv.at[k],
            device_id=(lax.rem(a + k, n_actor), m),
            device_id_type=MESH,
        )

    def to_mp(src, dst, send, recv, k):
        return pltpu.make_async_remote_copy(
            src_ref=src,
            dst_ref=dst,
            send_sem=send.at[k],
            recv_sem=recv.at[k],
            device_id=(a, lax.rem(m + k, n_mp)),
            device_id_type=MESH,
        )

    def start_all(copies):
        for copy in copies:
            copy.start()

    def wait_all(copies):
        for copy in copies:
            copy.wait()

    gathers = [to_actor(gbuf.at[0], gbuf.at[k], g_send, g_recv, k) for k in range(1, n_actor)]
    start_all(gathers)

    step = 128

    @pl.loop(0, norm_steps)
    def _(i):
        x_copy(i).wait()
        rows = pl.ds(pl.multiple_of(i * NORM_ROWS, NORM_ROWS), NORM_ROWS)
        total = jnp.zeros((NORM_ROWS, step), F32)
        for c in range(0, width, step):
            v = x[rows, c : c + step].astype(F32)
            total += v * v
        scale = lax.rsqrt(jnp.sum(total, axis=1, keepdims=True) * (1.0 / width) + 1e-05)
        scale = jnp.broadcast_to(scale, (NORM_ROWS, step))
        for c in range(0, width, step):
            v = x[rows, c : c + step].astype(F32)
            g = gain[:, c : c + step].astype(F32)
            x[rows, c : c + step] = (v * scale * g).astype(BF16)

    w_copy.wait()

    def multiply(first, last):
        @pl.loop(first, last)
        def _(i):
            rows = pl.ds(pl.multiple_of(i * seq, seq), seq)
            acc[rows] = jnp.dot(x[rows], w[...], preferred_element_type=F32)

    multiply(0, EARLY)
    cot_copy.wait()
    wait_all(gathers)

    for j in range(n_actor):
        tab[j * block : (j + 1) * block] = gbuf[lax.rem(a - owner[j] + n_actor, n_actor)]

    own_cols = pl.ds(pl.multiple_of(m * cols, cols), cols)

    @pl.loop(0, n_mp)
    def _(q):
        rows = pl.ds(pl.multiple_of(q * part, part), part)
        low_part = jnp.dot(x[rows, own_cols], tab[...], preferred_element_type=F32)
        back_part = jnp.dot(cot[rows], tab[...], preferred_element_type=F32)
        lane = lax.broadcasted_iota(jnp.int32, (part, lanes), 1)
        pbuf[q] = jnp.where(lane < rank, low_part, back_part).astype(BF16)

    sums = [
        to_mp(pbuf.at[lax.rem(m + k, n_mp)], rbuf.at[k], p_send, p_recv, k) for k in range(1, n_mp)
    ]
    start_all(sums)
    multiply(EARLY, MID)
    wait_all(sums)

    mine = pbuf[m].astype(F32)
    for k in range(1, n_mp):
        mine += rbuf[k].astype(F32)
    my_rows = pl.ds(pl.multiple_of(m * part, part), part)
    lb[my_rows] = jnp.where(live[my_rows] > 0.0, mine, 0.0).astype(BF16)
    spreads = [to_mp(lb.at[my_rows], lb.at[my_rows], l_send, l_recv, k) for k in range(1, n_mp)]
    start_all(spreads)
    multiply(MID, nseq)
    wait_all(spreads)

    rolled = pltpu.roll(lb[...].astype(F32), rank, 1)
    lbr[...] = rolled.astype(BF16)
    lbt = rolled.T.astype(BF16)
    down = jnp.dot(lbt, x[:, own_cols], preferred_element_type=F32)
    up = jnp.dot(lbt, cot[...], preferred_element_type=F32)
    row = lax.broadcasted_iota(jnp.int32, (lanes, cols), 0)
    grad[...] = (adapter_scale * jnp.where(row < rank, down, up)).T.reshape(n_actor, block, lanes)

    def position(actor):
        found = jnp.int32(0)
        for j in range(n_actor):
            found = jnp.where(owner[j] == actor, j, found)
        return found

    for k in range(1, n_actor):
        sbuf[k] = grad[position(lax.rem(a + k, n_actor))].astype(BF16)
    scatters = [to_actor(sbuf.at[k], rsbuf.at[k], s_send, s_recv, k) for k in range(1, n_actor)]
    start_all(scatters)

    tab_lane = lax.broadcasted_iota(jnp.int32, (cols, lanes), 1)
    gbuf_b = jnp.where(tab_lane >= rank, tab[...].astype(F32), 0.0).astype(BF16)
    fresh_b[...] = gbuf_b

    def q_copy(i):
        rows = pl.ds(pl.multiple_of(i * seq, seq), seq)
        return pltpu.make_async_copy(qbuf.at[rows], query.at[rows], q_sem.at[i])

    for i in range(nseq):
        rows = pl.ds(i * seq, seq)
        extra = lax.dot_general(
            lbr[rows], fresh_b[...], (((1,), (1,)), ((), ())), preferred_element_type=F32
        )
        alive = lax.broadcasted_iota(jnp.int32, (seq, cols), 0) < lengths[i]
        qbuf[rows] = jnp.where(alive, acc[rows] + adapter_scale * extra, 0.0).astype(BF16)
        q_copy(i).start()

    wait_all(scatters)
    total = grad[position(a)]
    for k in range(1, n_actor):
        total += rsbuf[k].astype(F32)
    first = beta_one * one[...] + (1.0 - beta_one) * total
    second = beta_two * two[...] + (1.0 - beta_two) * total * total
    updated = table[...] - learn_rate * (first / fix_one) / (jnp.sqrt(second / fix_two) + 1e-08)
    nbuf[0] = updated.astype(BF16)

    news = [to_actor(nbuf.at[0], nbuf.at[k], n_send, n_recv, k) for k in range(1, n_actor)]
    downs = []
    for e in range(share):
        target = m * share + e
        slot = lax.rem(target - a + n_actor, n_actor)
        for k in range(1, n_mp):
            downs.append(
                pltpu.make_async_remote_copy(
                    src_ref=nbuf.at[0],
                    dst_ref=abuf.at[slot],
                    send_sem=a_send.at[e * n_mp + k],
                    recv_sem=a_recv.at[slot],
                    device_id=(target, lax.rem(m + k, n_mp)),
                    device_id_type=MESH,
                )
            )
    start_all(news)
    start_all(downs)
    one_new[...] = first
    two_new[...] = second
    table_new[...] = updated

    wait_all(news)
    for copy in downs:
        copy.wait_send()
    source = a // share
    far = source != m

    @pl.when(far)
    def _():
        for k in range(n_actor):
            pltpu.make_async_remote_copy(
                src_ref=nbuf.at[0],
                dst_ref=abuf.at[k],
                send_sem=a_send.at[0],
                recv_sem=a_recv.at[k],
                device_id=(a, lax.rem(m + 1, n_mp)),
                device_id_type=MESH,
            ).wait_recv()

    @pl.when(source == m)
    def _():
        abuf[...] = nbuf[...]

    tail_lane = lax.broadcasted_iota(jnp.int32, (block, lanes), 1)
    for j in range(n_actor):
        block_now = nbuf[lax.rem(a - owner[j] + n_actor, n_actor)].astype(F32)
        turned = pltpu.roll(block_now, rank, 1)
        fresh_b[j * block : (j + 1) * block] = jnp.where(tail_lane < rank, turned, 0.0).astype(BF16)
    start = lax.rem(a, share) * n_mp
    for j in range(n_mp):
        fresh_a[j * block : (j + 1) * block] = abuf[
            lax.rem(a - owner[start + j] + n_actor, n_actor)
        ]
    extra = lax.dot_general(
        fresh_a[...], fresh_b[...], (((1,), (1,)), ((), ())), preferred_element_type=F32
    )
    base = w[pl.ds(pl.multiple_of(a * row_count, row_count), row_count)].astype(F32)
    mbuf[...] = (base + adapter_scale * extra).astype(BF16)
    m_copy = pltpu.make_async_copy(mbuf, merged, m_sem)
    m_copy.start()
    for i in range(nseq):
        q_copy(i).wait()
    m_copy.wait()


def body(
    resid, norm_gain, query_weight, cotangent, lengths, owner, adapter_table, moment_one, moment_two
):
    n_actor = lax.axis_size("actor")
    n_mp = lax.axis_size("mp")
    tokens, width = resid.shape
    cols = query_weight.shape[1]
    block, lanes = adapter_table.shape[2:]
    nseq = lengths.shape[0]
    row_count = width // n_actor
    part = tokens // n_mp
    flat = (block, lanes)
    smem = pl.BlockSpec(memory_space=pltpu.SMEM)
    vmem = pl.BlockSpec(memory_space=pltpu.VMEM)
    hbm = pl.BlockSpec(memory_space=pl.ANY)
    dma = pltpu.SemaphoreType.DMA
    query, updated, first, second, merged = pl.pallas_call(
        functools.partial(kernel, n_actor, n_mp),
        out_shape=(
            jax.ShapeDtypeStruct((tokens, cols), BF16),
            jax.ShapeDtypeStruct(flat, F32),
            jax.ShapeDtypeStruct(flat, F32),
            jax.ShapeDtypeStruct(flat, F32),
            jax.ShapeDtypeStruct((row_count, cols), BF16),
        ),
        in_specs=[smem, smem, vmem, vmem, vmem, vmem, hbm, hbm, hbm],
        out_specs=(hbm, vmem, vmem, vmem, hbm),
        scratch_shapes=[
            pltpu.VMEM((tokens, width), BF16),
            pltpu.VMEM((width, cols), BF16),
            pltpu.VMEM((tokens, cols), BF16),
            pltpu.VMEM((tokens, cols), F32),
            pltpu.VMEM((tokens, cols), BF16),
            pltpu.VMEM((row_count, cols), BF16),
            pltpu.VMEM((tokens, lanes), F32),
            pltpu.VMEM((n_actor, block, lanes), BF16),
            pltpu.VMEM((cols, lanes), BF16),
            pltpu.VMEM((n_mp, part, lanes), BF16),
            pltpu.VMEM((n_mp, part, lanes), BF16),
            pltpu.VMEM((tokens, lanes), BF16),
            pltpu.VMEM((tokens, lanes), BF16),
            pltpu.VMEM((n_actor, block, lanes), F32),
            pltpu.VMEM((n_actor, block, lanes), BF16),
            pltpu.VMEM((n_actor, block, lanes), BF16),
            pltpu.VMEM((n_actor, block, lanes), BF16),
            pltpu.VMEM((n_actor, block, lanes), BF16),
            pltpu.VMEM((cols, lanes), BF16),
            pltpu.VMEM((row_count, lanes), BF16),
            dma((tokens // NORM_ROWS,)),
            dma,
            dma,
            dma((nseq,)),
            dma,
            dma((n_actor,)),
            dma((n_actor,)),
            dma((n_mp,)),
            dma((n_mp,)),
            dma((n_mp,)),
            dma((n_mp,)),
            dma((n_actor,)),
            dma((n_actor,)),
            dma((n_actor,)),
            dma((n_actor,)),
            dma((n_actor,)),
            dma((n_actor,)),
        ],
        compiler_params=pltpu.CompilerParams(
            collective_id=0, has_side_effects=True, vmem_limit_bytes=56 * 2**20
        ),
    )(
        lengths,
        owner,
        norm_gain.reshape(1, width),
        adapter_table.reshape(flat),
        moment_one.reshape(flat),
        moment_two.reshape(flat),
        resid,
        query_weight,
        cotangent,
    )
    shape = adapter_table.shape
    return (query, updated.reshape(shape), first.reshape(shape), second.reshape(shape), merged)


def solution(mesh):
    return jax.shard_map(
        body,
        mesh=mesh,
        in_specs=(
            P("actor", None),
            P(),
            P(None, "mp"),
            P("actor", "mp"),
            P("actor"),
            P(),
            P("mp", "actor", None, None),
            P("mp", "actor", None, None),
            P("mp", "actor", None, None),
        ),
        out_specs=(
            P("actor", "mp"),
            P("mp", "actor", None, None),
            P("mp", "actor", None, None),
            P("mp", "actor", None, None),
            P("actor", "mp"),
        ),
        check_vma=False,
    )
```

time: 218 us -> 60 us (0.28)
  the two profiles are of different devices: /device:TPU:0 before, /device:TPU:7 now
where the time goes in v1:
time: 60 us; the launch traced here: 59.8 us
  Pallas kernels  51.8 us (86%)
  local copies, waits for them, and re-layouts  7.36 us (12%)
  between operations  0.68 us (1%)
    pallas_call x1, Pallas kernels, body(): pl.pallas_call(functools.partial(kernel, n_actor, n_mp), out_shape=(jax.S...  51.8 us
    unnamed x13, local copies, waits for them, and re-layouts  6.05 us
    reshape x1, local copies, waits for them, and re-layouts, body(): norm_gain.reshape(1, width)  1.31 us

profile of v1, /device:TPU:7, one launch (start us, length us, event | category | flops | bytes accessed | tf_op | source)
XLA Modules:
  0.0 59.8 jit_solution(2263287424442865772)
XLA Ops:
  0.6 1.3 %reshape.31.gain = bf16[1,4096]{1,0:T(2,128)(2,1)} reshape(bf16[4096]{0:T(1024)(128)(2,1)} %param.10) | data formatting | bytes 16384 | tf_op jit(solution)/shard_map/reshape | solution.py:398
  1.9 51.8 %shard_map.128 = (bf16[1024,1024]{1,0:T(8,128)(2,1)}, f32[128,128]{1,0:T(8,128)}, f32[128,128]{1,0:T(8,128)}, f32[128,128]{1,0:T(8,128)}, bf16[512,1024]{1,0:T(8,128)(2,1)}) custom-call(s32[4]{0:T(128)} %lengths.1, s32[8]{0:T(128)} %owner.1, bf16[1,4096]{1,0:T(2,128)(2,1)} %reshape.31.gain, f32[128,128]{1,0:T(8,128)} %bitcast.6, f32[128,128]{1,0:T(8,128)} %bitcast.7, ...), custom_call_target="tpu_custom_call" | custom-call | tf_op jit(solution)/shard_map/pallas_call | solution.py:342
  53.7 0.0 copy-start.3
  53.7 0.0 copy-start.2
  53.7 0.0 copy-start.1
  53.7 0.0 copy-start
  53.7 3.2 %copy.19 = bf16[1024,1024]{1,0:T(8,128)(2,1)} copy(bf16[1024,1024]{1,0:T(8,128)(2,1)} %get-tuple-element.20) | data formatting | bytes 4194304
  56.9 0.0 copy-done.3
  56.9 0.6 %copy.20 = f32[1,1,128,128]{3,2,1,0:T(8,128)} copy(f32[1,1,128,128]{3,2,1,0:T(8,128)S(1)} %bitcast.11) | data formatting | bytes 131072
  57.6 0.0 copy-done.2
  57.6 0.6 %copy.21 = f32[1,1,128,128]{3,2,1,0:T(8,128)} copy(f32[1,1,128,128]{3,2,1,0:T(8,128)S(1)} %bitcast.10) | data formatting | bytes 131072
  58.2 0.0 copy-done.1
  58.2 0.6 %copy.22 = f32[1,1,128,128]{3,2,1,0:T(8,128)} copy(f32[1,1,128,128]{3,2,1,0:T(8,128)S(1)} %bitcast.9) | data formatting | bytes 131072
  58.8 0.0 copy-done
  58.8 1.0 %copy.23 = bf16[512,1024]{1,0:T(8,128)(2,1)} copy(bf16[512,1024]{1,0:T(8,128)(2,1)S(1)} %copy-done) | data formatting | bytes 2097152
Async XLA Ops:
  53.7 3.2 %copy-start.3 = (f32[128,128]{1,0:T(8,128)S(1)}, f32[128,128]{1,0:T(8,128)}, u32[]{:S(2)}) copy-start(f32[128,128]{1,0:T(8,128)} %get-tuple-element.11) | copy-start | bytes 196612
  53.7 3.8 %copy-start.2 = (f32[128,128]{1,0:T(8,128)S(1)}, f32[128,128]{1,0:T(8,128)}, u32[]{:S(2)}) copy-start(f32[128,128]{1,0:T(8,128)} %get-tuple-element.12) | copy-start | bytes 196612
  53.7 4.5 %copy-start.1 = (f32[128,128]{1,0:T(8,128)S(1)}, f32[128,128]{1,0:T(8,128)}, u32[]{:S(2)}) copy-start(f32[128,128]{1,0:T(8,128)} %get-tuple-element.13) | copy-start | bytes 196612
  53.7 5.1 %copy-start = (bf16[512,1024]{1,0:T(8,128)(2,1)S(1)}, bf16[512,1024]{1,0:T(8,128)(2,1)}, u32[]{:S(2)}) copy-start(bf16[512,1024]{1,0:T(8,128)(2,1)} %get-tuple-element.24) | copy-start | bytes 3145732

commit v2 on v1

--- a/solution.py
+++ b/solution.py
@@ -44,8 +44,6 @@
     w,
     cot,
     acc,
-    qbuf,
-    mbuf,
     live,
     gbuf,
     tab,
@@ -60,11 +58,11 @@
     abuf,
     fresh_b,
     fresh_a,
+    gain_row,
+    asrc,
     x_sem,
     w_sem,
     cot_sem,
-    q_sem,
-    m_sem,
     g_send,
     g_recv,
     p_send,
@@ -154,6 +152,7 @@
     start_all(gathers)
 
     step = 128
+    gain_row[...] = gain[...].astype(F32).reshape(1, width)
 
     @pl.loop(0, norm_steps)
     def _(i):
@@ -167,7 +166,7 @@
         scale = jnp.broadcast_to(scale, (NORM_ROWS, step))
         for c in range(0, width, step):
             v = x[rows, c : c + step].astype(F32)
-            g = gain[:, c : c + step].astype(F32)
+            g = gain_row[:, c : c + step]
             x[rows, c : c + step] = (v * scale * g).astype(BF16)
 
     w_copy.wait()
@@ -235,18 +234,13 @@
     gbuf_b = jnp.where(tab_lane >= rank, tab[...].astype(F32), 0.0).astype(BF16)
     fresh_b[...] = gbuf_b
 
-    def q_copy(i):
-        rows = pl.ds(pl.multiple_of(i * seq, seq), seq)
-        return pltpu.make_async_copy(qbuf.at[rows], query.at[rows], q_sem.at[i])
-
     for i in range(nseq):
         rows = pl.ds(i * seq, seq)
         extra = lax.dot_general(
             lbr[rows], fresh_b[...], (((1,), (1,)), ((), ())), preferred_element_type=F32
         )
         alive = lax.broadcasted_iota(jnp.int32, (seq, cols), 0) < lengths[i]
-        qbuf[rows] = jnp.where(alive, acc[rows] + adapter_scale * extra, 0.0).astype(BF16)
-        q_copy(i).start()
+        query[rows] = jnp.where(alive, acc[rows] + adapter_scale * extra, 0.0).astype(BF16)
 
     wait_all(scatters)
     total = grad[position(a)]
@@ -255,72 +249,101 @@
     first = beta_one * one[...] + (1.0 - beta_one) * total
     second = beta_two * two[...] + (1.0 - beta_two) * total * total
     updated = table[...] - learn_rate * (first / fix_one) / (jnp.sqrt(second / fix_two) + 1e-08)
-    nbuf[0] = updated.astype(BF16)
-
-    news = [to_actor(nbuf.at[0], nbuf.at[k], n_send, n_recv, k) for k in range(1, n_actor)]
-    downs = []
-    for e in range(share):
+    half = block // 2
+    top, bottom = updated[:half], updated[half:]
+    left = lax.broadcasted_iota(jnp.int32, (half, lanes), 1) < rank
+    asrc[...] = jnp.where(left, top, pltpu.roll(bottom, rank, 1)).astype(BF16)
+    nbuf[0] = jnp.where(left, pltpu.roll(top, rank, 1), bottom).astype(BF16)
+
+    source = a // share
+
+    def down(e, k):
         target = m * share + e
         slot = lax.rem(target - a + n_actor, n_actor)
+        return pltpu.make_async_remote_copy(
+            src_ref=asrc,
+            dst_ref=abuf.at[slot],
+            send_sem=a_send.at[e * n_mp + k],
+            recv_sem=a_recv.at[slot],
+            device_id=(target, lax.rem(m + k, n_mp)),
+            device_id_type=MESH,
+        )
+
+    news = [to_actor(nbuf.at[0], nbuf.at[k], n_send, n_recv, k) for k in range(1, n_actor)]
+    for e in range(share):
         for k in range(1, n_mp):
-            downs.append(
-                pltpu.make_async_remote_copy(
-                    src_ref=nbuf.at[0],
-                    dst_ref=abuf.at[slot],
-                    send_sem=a_send.at[e * n_mp + k],
-                    recv_sem=a_recv.at[slot],
-                    device_id=(target, lax.rem(m + k, n_mp)),
-                    device_id_type=MESH,
-                )
-            )
+            down(e, k).start()
+
+        @pl.when(m * share + e != a)
+        def _():
+            down(e, 0).start()
+
     start_all(news)
-    start_all(downs)
+
+    @pl.when(source == m)
+    def _():
+        abuf[0] = asrc[...]
+
     one_new[...] = first
     two_new[...] = second
     table_new[...] = updated
 
+    def arrived(k):
+        pltpu.make_async_remote_copy(
+            src_ref=asrc,
+            dst_ref=abuf.at[k],
+            send_sem=a_send.at[0],
+            recv_sem=a_recv.at[k],
+            device_id=(a, lax.rem(m + 1, n_mp)),
+            device_id_type=MESH,
+        ).wait_recv()
+
+    for k in range(1, n_actor):
+        arrived(k)
+
+    @pl.when(source != m)
+    def _():
+        arrived(0)
+
     wait_all(news)
-    for copy in downs:
-        copy.wait_send()
-    source = a // share
-    far = source != m
-
-    @pl.when(far)
-    def _():
-        for k in range(n_actor):
-            pltpu.make_async_remote_copy(
-                src_ref=nbuf.at[0],
-                dst_ref=abuf.at[k],
-                send_sem=a_send.at[0],
-                recv_sem=a_recv.at[k],
-                device_id=(a, lax.rem(m + 1, n_mp)),
-                device_id_type=MESH,
-            ).wait_recv()
-
-    @pl.when(source == m)
-    def _():
-        abuf[...] = nbuf[...]
-
-    tail_lane = lax.broadcasted_iota(jnp.int32, (block, lanes), 1)
+    for e in range(share):
+        for k in range(1, n_mp):
+            down(e, k).wait_send()
+
+        @pl.when(m * share + e != a)
+        def _():
+            down(e, 0).wait_send()
+
     for j in range(n_actor):
-        block_now = nbuf[lax.rem(a - owner[j] + n_actor, n_actor)].astype(F32)
-        turned = pltpu.roll(block_now, rank, 1)
-        fresh_b[j * block : (j + 1) * block] = jnp.where(tail_lane < rank, turned, 0.0).astype(BF16)
+        packed = nbuf[lax.rem(a - owner[j] + n_actor, n_actor)].astype(F32)
+        rows = j * block
+        fresh_b[rows : rows + half] = jnp.where(left, packed, 0.0).astype(BF16)
+        fresh_b[rows + half : rows + block] = jnp.where(
+            left, pltpu.roll(packed, rank, 1), 0.0
+        ).astype(BF16)
     start = lax.rem(a, share) * n_mp
     for j in range(n_mp):
-        fresh_a[j * block : (j + 1) * block] = abuf[
-            lax.rem(a - owner[start + j] + n_actor, n_actor)
-        ]
+        packed = abuf[lax.rem(a - owner[start + j] + n_actor, n_actor)].astype(F32)
+        rows = j * block
+        fresh_a[rows : rows + half] = packed.astype(BF16)
+        fresh_a[rows + half : rows + block] = pltpu.roll(packed, rank, 1).astype(BF16)
     extra = lax.dot_general(
         fresh_a[...], fresh_b[...], (((1,), (1,)), ((), ())), preferred_element_type=F32
     )
     base = w[pl.ds(pl.multiple_of(a * row_count, row_count), row_count)].astype(F32)
-    mbuf[...] = (base + adapter_scale * extra).astype(BF16)
-    m_copy = pltpu.make_async_copy(mbuf, merged, m_sem)
-    m_copy.start()
-    for i in range(nseq):
-        q_copy(i).wait()
-    m_copy.wait()
+    merged[...] = (base + adapter_scale * extra).astype(BF16)
+
+
+def put_out(*refs):
+    count = len(refs) // 2
+    sems = refs[-1]
+    copies = [
+        pltpu.make_async_copy(refs[i], refs[count + i], sems.at[i]) for i in range(count)
+    ]
+    for copy in copies:
+        copy.start()
+    for copy in copies:
+        copy.wait()
 
 
 def body(
@@ -339,24 +362,23 @@
     vmem = pl.BlockSpec(memory_space=pltpu.VMEM)
     hbm = pl.BlockSpec(memory_space=pl.ANY)
     dma = pltpu.SemaphoreType.DMA
-    query, updated, first, second, merged = pl.pallas_call(
+    shapes = (
+        ((tokens, cols), BF16),
+        (flat, F32),
+        (flat, F32),
+        (flat, F32),
+        ((row_count, cols), BF16),
+    )
+    results = pl.pallas_call(
         functools.partial(kernel, n_actor, n_mp),
-        out_shape=(
-            jax.ShapeDtypeStruct((tokens, cols), BF16),
-            jax.ShapeDtypeStruct(flat, F32),
-            jax.ShapeDtypeStruct(flat, F32),
-            jax.ShapeDtypeStruct(flat, F32),
-            jax.ShapeDtypeStruct((row_count, cols), BF16),
-        ),
+        out_shape=tuple(pltpu.VMEM(shape, dtype) for shape, dtype in shapes),
         in_specs=[smem, smem, vmem, vmem, vmem, vmem, hbm, hbm, hbm],
-        out_specs=(hbm, vmem, vmem, vmem, hbm),
+        out_specs=(vmem,) * len(shapes),
         scratch_shapes=[
             pltpu.VMEM((tokens, width), BF16),
             pltpu.VMEM((width, cols), BF16),
             pltpu.VMEM((tokens, cols), BF16),
             pltpu.VMEM((tokens, cols), F32),
-            pltpu.VMEM((tokens, cols), BF16),
-            pltpu.VMEM((row_count, cols), BF16),
             pltpu.VMEM((tokens, lanes), F32),
             pltpu.VMEM((n_actor, block, lanes), BF16),
             pltpu.VMEM((cols, lanes), BF16),
@@ -367,14 +389,14 @@
             pltpu.VMEM((n_actor, block, lanes), F32),
             pltpu.VMEM((n_actor, block, lanes), BF16),
             pltpu.VMEM((n_actor, block, lanes), BF16),
-            pltpu.VMEM((n_actor, block, lanes), BF16),
-            pltpu.VMEM((n_actor, block, lanes), BF16),
+            pltpu.VMEM((n_actor, block // 2, lanes), BF16),
+            pltpu.VMEM((n_actor, block // 2, lanes), BF16),
             pltpu.VMEM((cols, lanes), BF16),
             pltpu.VMEM((row_count, lanes), BF16),
+            pltpu.VMEM((1, width), F32),
+            pltpu.VMEM((block // 2, lanes), BF16),
             dma((tokens // NORM_ROWS,)),
             dma,
-            dma,
-            dma((nseq,)),
             dma,
             dma((n_actor,)),
             dma((n_actor,)),
@@ -395,7 +417,7 @@
     )(
         lengths,
         owner,
-        norm_gain.reshape(1, width),
+        norm_gain,
         adapter_table.reshape(flat),
         moment_one.reshape(flat),
         moment_two.reshape(flat),
@@ -403,6 +425,14 @@
         query_weight,
         cotangent,
     )
+    query, updated, first, second, merged = pl.pallas_call(
+        put_out,
+        out_shape=tuple(jax.ShapeDtypeStruct(shape, dtype) for shape, dtype in shapes),
+        in_specs=[vmem] * len(shapes),
+        out_specs=(hbm,) * len(shapes),
+        scratch_shapes=[dma((len(shapes),))],
+        compiler_params=pltpu.CompilerParams(vmem_limit_bytes=2**20),
+    )(*results)
     shape = adapter_table.shape
     return (query, updated.reshape(shape), first.reshape(shape), second.reshape(shape), merged)
 

time: 60 us -> 48.4 us (0.81)
  the two profiles are of different devices: /device:TPU:7 before, /device:TPU:0 now
where the time goes in v2:
time: 48.4 us; the launch traced here: 48.2 us
  Pallas kernels  47.6 us (98%)
  between operations  0.64 us (1%)
    pallas_call x1, Pallas kernels, body(): pl.pallas_call(functools.partial(kernel, n_actor, n_mp), out_shape=tuple(...  45.8 us
    pallas_call x1, Pallas kernels, body(): pl.pallas_call(put_out, out_shape=tuple((jax.ShapeDtypeStruct(shape, dtyp...  1.77 us

profile of v2, /device:TPU:0, one launch (start us, length us, event | category | flops | bytes accessed | tf_op | source)
XLA Modules:
  0.0 48.2 jit_solution(8100143454925312770)
XLA Ops:
  0.6 45.8 %shard_map.128 = (bf16[1024,1024]{1,0:T(8,128)(2,1)S(1)}, f32[128,128]{1,0:T(8,128)S(1)}, f32[128,128]{1,0:T(8,128)S(1)}, f32[128,128]{1,0:T(8,128)S(1)}, bf16[512,1024]{1,0:T(8,128)(2,1)S(1)}) custom-call(s32[4]{0:T(128)} %lengths.1, s32[8]{0:T(128)} %owner.1, bf16[4096]{0:T(1024)(128)(2,1)} %gain.1, f32[128,128]{1,0:T(8,128)} %bitcast.6, ...), custom_call_target="tpu_custom_call" | custom-call | tf_op jit(solution)/shard_map/pallas_call | solution.py:372
  46.4 1.8 %shard_map.129 = (bf16[1024,1024]{1,0:T(8,128)(2,1)}, f32[128,128]{1,0:T(8,128)}, f32[128,128]{1,0:T(8,128)}, f32[128,128]{1,0:T(8,128)}, bf16[512,1024]{1,0:T(8,128)(2,1)}) custom-call(bf16[1024,1024]{1,0:T(8,128)(2,1)S(1)} %get-tuple-element.15.refs_0_, f32[128,128]{1,0:T(8,128)S(1)} %get-tuple-element.16.refs_1_, ...), custom_call_target="tpu_custom_call" | custom-call | tf_op jit(solution)/shard_map/pallas_call | solution.py:428
